TPU v7x, 32 devices: a whole 2x2x4 slice. The times are simulated.
32 devices in a mesh: outer: 4 (over y, x), dev: 8 (over z, core).
Axes of the slice: x: 2, y: 2, z: 4, core: 2. Of those that a mesh axis runs over, the one named last changes fastest.
Arguments:
- documents: bfloat16 [6144, 4096], P(('outer', 'dev')), may hold values from -8 to 8
- cluster_of: int32 [6144], replicated, may hold values from 0 to 31, as said below
- neighbours: int32 [32, 4], replicated, may hold values from 0 to 31, as said below
- sharpness: float32 [32], replicated, may hold values from 32 to 64
Outputs:
- density: float32 [6144], P(('outer', 'dev'))
Inputs may be any that keep to these rules, and one draw needn't show every extreme that they name: `cluster_of`: rows b * 192 to (b + 1) * 192 - 1 form block b. Block b names only clusters g * 8 to (g + 1) * 8 - 1, with g = b // 8, and names no cluster more than 48 times; in each group g some cluster is named exactly 48 times by every block of that group; every cluster is named by some row. `neighbours`: row c, with c = g * 8 + h, lists in order the clusters g * 8 + ((h - 1) mod 8), g * 8 + ((h + 1) mod 8), ((g - 1) mod 4) * 8 + ((h + b) mod 8) and ((g + 1) mod 4) * 8 + ((h + d) mod 8), with b and d each in -1, 0, 1.
All inputs are finite; a program needn't handle non-finite values.
Results may differ from a plain program's by a relative error of at most 0.00047.
Values may be sent and summed in bfloat16 or wider, within the bound.
A program may use at most 128 MiB of HBM per device.

v0:
```python
import functools
import math

import jax
import jax.numpy as jnp
from jax import lax
from jax.experimental import pallas as pl
from jax.experimental.pallas import tpu as pltpu
from jax.sharding import PartitionSpec as P


def passed_along(block, axis, distance):
    devices = range(lax.axis_size(axis))
    route = [((i - distance) % len(devices), i) for i in devices]
    return lax.ppermute(block, axis, route)


def kernel_block(queries, others, pair_gain):
    products = jnp.einsum("qe,ke->qk", queries, others, preferred_element_type=jnp.float32)
    return jnp.exp(pair_gain * products)


def shards(documents, cluster_of, neighbours, sharpness):
    groups = lax.axis_size("outer")
    owners = lax.axis_size("dev")
    tokens_here = documents.shape[0]
    feature_width = documents.shape[1]
    capacity = max(2, 2 * tokens_here // owners)
    slot_count = owners * capacity
    group_index = lax.axis_index("outer")
    owner_index = lax.axis_index("dev")
    own_cluster = group_index * owners + owner_index
    block_labels = cluster_of.reshape(groups * owners, tokens_here)
    group_of_block = jnp.arange(groups * owners, dtype=jnp.int32) // owners
    local_labels = block_labels - group_of_block[:, None] * owners
    owner_range = jnp.arange(owners, dtype=jnp.int32)
    per_block = jnp.sum(
        (local_labels[:, :, None] == owner_range).astype(jnp.int32), axis=1
    ).reshape(groups, owners, owners)
    cluster_sizes = jnp.sum(per_block, axis=1).reshape(-1)
    own_labels = lax.dynamic_index_in_dim(local_labels, own_cluster, 0, keepdims=False)
    ordinal = jnp.arange(tokens_here, dtype=jnp.int32)
    earlier = ordinal[None, :] < ordinal[:, None]
    repeats = jnp.sum(
        ((own_labels[:, None] == own_labels[None, :]) & earlier).astype(jnp.int32), axis=1
    )
    target = own_labels * capacity + repeats
    placing = (jnp.arange(slot_count, dtype=jnp.int32)[:, None] == target[None, :]).astype(
        jnp.bfloat16
    )
    outgoing = jnp.dot(placing, documents, preferred_element_type=jnp.float32).astype(jnp.bfloat16)
    arrived = lax.all_to_all(
        outgoing.reshape(owners, capacity, feature_width),
        "dev",
        split_axis=0,
        concat_axis=0,
        tiled=True,
    ).reshape(slot_count, feature_width)

    def slot_mask(group_at, owner_at):
        senders = per_block[group_at, :, owner_at]
        return (
            (jnp.arange(capacity, dtype=jnp.int32)[None, :] < senders[:, None])
            .astype(jnp.float32)
            .reshape(-1)
        )

    present = slot_mask(group_index, owner_index)
    centre = jnp.dot(
        present.astype(jnp.bfloat16)[None, :], arrived, preferred_element_type=jnp.float32
    )[0]
    centre = centre / cluster_sizes[own_cluster].astype(jnp.float32)
    centred = arrived.astype(jnp.float32) - centre[None, :]
    scaling = lax.rsqrt(jnp.mean(centred * centred, axis=1) + 1e-06) / math.sqrt(feature_width)
    unit_rows = (centred * (scaling * present)[:, None]).astype(jnp.bfloat16)
    own_gain = sharpness[own_cluster]
    listed = neighbours[own_cluster]
    off_diagonal = 1.0 - jnp.eye(slot_count, dtype=jnp.float32)
    running = jnp.sum(
        kernel_block(unit_rows, unit_rows, own_gain) * (present[None, :] * off_diagonal), axis=1
    )
    beside = [passed_along(unit_rows, "dev", offset) for offset in (1, -1)]
    vertical = []
    for direction, position in ((1, 2), (-1, 3)):
        receiver_group = (group_index + direction) % groups
        wanted = neighbours[receiver_group * owners + owner_index, position]
        delta = (wanted % owners - owner_index + owners) % owners
        picked_rows = jnp.where(
            delta == 1, beside[1], jnp.where(delta == owners - 1, beside[0], unit_rows)
        )
        vertical.append(passed_along(picked_rows, "outer", direction))
    key_sets = [beside[0], beside[1], vertical[0], vertical[1]]
    for position in range(4):
        partner = listed[position]
        partner_group_at = partner // owners
        partner_owner_at = partner % owners
        partner_partner = partner_group_at * owners + partner_owner_at
        pair_gain = 0.5 * (own_gain + sharpness[partner_partner])
        partner = partner_partner
        kernel_terms = kernel_block(unit_rows, key_sets[position], pair_gain)
        key_mask = slot_mask(partner_group_at, partner_owner_at)
        running = running + jnp.sum(kernel_terms * key_mask[None, :], axis=1)
    partner_count = cluster_sizes[own_cluster] - 1 + jnp.sum(cluster_sizes[listed])
    slot_density = jnp.log(running / partner_count.astype(jnp.float32))
    answered = lax.all_to_all(
        slot_density.reshape(owners, capacity), "dev", split_axis=0, concat_axis=0, tiled=True
    ).reshape(-1)
    return answered[target]


MESH = pl.DeviceIdType.MESH


def meet(peers, expected):
    barrier = pltpu.get_barrier_semaphore()
    for present, peer in peers:
        if present is None:
            pl.semaphore_signal(barrier, inc=1, device_id=peer, device_id_type=MESH)
        else:

            @pl.when(present)
            def _(peer=peer):
                pl.semaphore_signal(barrier, inc=1, device_id=peer, device_id_type=MESH)

    pl.semaphore_wait(barrier, expected)


def sum_kernel(owners, part_ref, out_ref, landed, reduced, gathered_sums, sems):
    me = lax.axis_index("dev")
    width = part_ref.shape[1] // owners

    def span(at):
        return pl.ds(pl.multiple_of(at * width, 128), width)

    others = [lax.rem(me + step, owners) for step in range(1, owners)]
    meet([(None, {"dev": peer}) for peer in others], owners - 1)

    def scatter(step):
        return pltpu.make_async_remote_copy(
            src_ref=part_ref.at[:, span(others[step])],
            dst_ref=landed.at[step],
            send_sem=sems.at[0, step],
            recv_sem=sems.at[1, step],
            device_id={"dev": others[step]},
            device_id_type=MESH,
        )

    def spread(step):
        return pltpu.make_async_remote_copy(
            src_ref=reduced,
            dst_ref=gathered_sums.at[step],
            send_sem=sems.at[2, step],
            recv_sem=sems.at[3, step],
            device_id={"dev": others[step]},
            device_id_type=MESH,
        )

    for step in range(owners - 1):
        scatter(step).start()
    total = part_ref[:, span(me)]
    for step in range(owners - 1):
        scatter(step).wait_recv()
        total = total + landed[step]
    reduced[...] = total
    for step in range(owners - 1):
        spread(step).start()
    out_ref[:, span(me)] = total
    for step in range(owners - 1):
        spread(step).wait_recv()
        sender = lax.rem(me + owners - 1 - step, owners)
        out_ref[:, span(sender)] = gathered_sums[step]
    for step in range(owners - 1):
        scatter(step).wait_send()
        spread(step).wait_send()


def summed(part):
    owners = lax.axis_size("dev")
    rows, width = part.shape
    block = (owners - 1, rows, width // owners)
    return pl.pallas_call(
        functools.partial(sum_kernel, owners),
        out_shape=jax.ShapeDtypeStruct(part.shape, jnp.float32),
        in_specs=[pl.BlockSpec(memory_space=pltpu.VMEM)],
        out_specs=pl.BlockSpec(memory_space=pltpu.VMEM),
        scratch_shapes=[
            pltpu.VMEM(block, jnp.float32),
            pltpu.VMEM(block[1:], jnp.float32),
            pltpu.VMEM(block, jnp.float32),
            pltpu.SemaphoreType.DMA((4, owners - 1)),
        ],
        compiler_params=pltpu.CompilerParams(collective_id=0, has_side_effects=True),
        name="mean_sums",
    )(part)


def return_kernel(owners, cols_ref, rows_ref, out_ref, landed, sems):
    me = lax.axis_index("dev")
    group = lax.axis_index("outer")
    beside = group + 1 - 2 * lax.rem(group, 2)
    opposite = 3 - group
    others = [lax.rem(me + step, owners) for step in range(1, owners)]
    peers = [{"dev": peer} for peer in others] + [{"outer": beside}, {"outer": opposite}]
    sources = [cols_ref.at[peer] for peer in others] + [rows_ref.at[1], rows_ref.at[2]]
    meet([(None, peer) for peer in peers], len(peers))
    copies = [
        pltpu.make_async_remote_copy(
            src_ref=sources[k],
            dst_ref=landed.at[k],
            send_sem=sems.at[0, k],
            recv_sem=sems.at[1, k],
            device_id=peers[k],
            device_id_type=MESH,
        )
        for k in range(len(peers))
    ]
    for copy in copies:
        copy.start()
    total = rows_ref[0]
    for k, copy in enumerate(copies):
        copy.wait_recv()
        total = total + landed[k]
    out_ref[...] = total
    for copy in copies:
        copy.wait_send()


def returned(cols, rows):
    owners = lax.axis_size("dev")
    peers = owners + 1
    return pl.pallas_call(
        functools.partial(return_kernel, owners),
        out_shape=jax.ShapeDtypeStruct(cols.shape[1:], jnp.float32),
        in_specs=[pl.BlockSpec(memory_space=pltpu.VMEM)] * 2,
        out_specs=pl.BlockSpec(memory_space=pltpu.VMEM),
        scratch_shapes=[
            pltpu.VMEM((peers,) + cols.shape[1:], jnp.float32),
            pltpu.SemaphoreType.DMA((2, peers)),
        ],
        compiler_params=pltpu.CompilerParams(collective_id=2, has_side_effects=True),
        name="return_sums",
    )(cols, rows)


PIECES = 6


def pair_kernel(
    unit_ref, labels_ref, neighbours_ref, sharpness_ref, rows_ref, cols_ref,
    lists_ref, gain_ref, klist_ref, kgain_ref, acc_ref,
    queries, keys, z_sems, core_sems, key_sems, side_sems,
):
    dev = lax.axis_index("dev")
    group = lax.axis_index("outer")
    z, core = dev // 2, lax.rem(dev, 2)
    rows = unit_ref.shape[0]
    piece = rows // PIECES
    partner = {"dev": 2 * z + 1 - core}
    above = {"dev": lax.rem(dev + 2, 8)}
    below = {"dev": lax.rem(dev + 6, 8)}
    beside = {"outer": group + 1 - 2 * lax.rem(group, 2)}
    across = {"outer": lax.rem(group + 2, 4)}
    meet(
        [(None, partner), (None, beside), (None, across), (z < 3, above), (z > 0, below)],
        3 + jnp.where(z < 3, 1, 0) + jnp.where(z > 0, 1, 0),
    )

    def part(k):
        return pl.ds(pl.multiple_of(k * piece, piece), piece)

    def remote(src, dst, send_sem, recv_sem, device):
        return pltpu.make_async_remote_copy(
            src_ref=src, dst_ref=dst, send_sem=send_sem, recv_sem=recv_sem,
            device_id=device, device_id_type=MESH,
        )

    def hop(unit, k, device, own=False):
        at = 2 * unit + core
        src = unit_ref.at[part(k)] if own else keys.at[at, part(k)]
        return remote(src, keys.at[at, part(k)], z_sems.at[unit, k], key_sems.at[at, k], device)

    def share(unit, k, own=False):
        at = 2 * unit + core
        src = unit_ref.at[part(k)] if own else keys.at[at, part(k)]
        return remote(
            src, keys.at[at, part(k)], core_sems.at[unit, k], key_sems.at[at, k], partner
        )

    def side(k):
        return remote(
            unit_ref.at[part(k)], queries.at[1, part(k)],
            side_sems.at[0, k], side_sems.at[1, k], beside,
        )

    def relay(k):
        return remote(
            queries.at[1, part(k)], queries.at[2, part(k)],
            side_sems.at[2, k], side_sems.at[3, k], across,
        )

    def arrived(at, k):
        remote(
            keys.at[at, part(k)], keys.at[at, part(k)],
            core_sems.at[0, k], key_sems.at[at, k], partner,
        ).wait_recv()

    def own_sends(k, act):
        act(side(k))

        @pl.when(z < 2)
        def _():
            act(hop(z, k, above, own=True))

        @pl.when(z == 3)
        def _():
            act(hop(z, k, below, own=True))

        act(share(z, k, own=True))

    def start(copy):
        copy.start()

    def sent(copy):
        copy.wait_send()

    def loop(body):
        lax.fori_loop(0, PIECES, lambda k, carry: (body(k), carry)[1], 0)

    loop(lambda k: own_sends(k, start))
    square = (rows, rows)
    same = lax.broadcasted_iota(jnp.int32, square, 0) == lax.broadcasted_iota(jnp.int32, square, 1)

    def chosen(read, labels, base, zero):
        found = jnp.full(labels.shape, zero, jnp.float32)
        for h in range(8):
            found = jnp.where(labels == base + h, read(base + h), found)
        return found

    def listed(position):
        return lambda c: neighbours_ref[c, position].astype(jnp.float32)

    def sharp(c):
        return sharpness_ref[c]

    def upright(row):
        return jnp.sum(jnp.where(same, row, 0.0), axis=1, keepdims=True)

    odd = lax.rem(group, 2)
    toward = {0: None, 1: 2 + odd, 2: 3 - odd}
    for b, at_group in enumerate((group, group + 1 - 2 * odd, 3 - group)):
        base = at_group * 8
        labels = labels_ref[base + dev]
        lists_ref[b, 0] = upright(labels.astype(jnp.float32))
        gain_ref[b] = upright(chosen(sharp, labels, base, 0.0))
        positions = (0, 1) if b == 0 else (toward[b],)
        for slot, position in enumerate(positions):
            lists_ref[b, 1 + slot] = upright(chosen(listed(position), labels, base, 0.0))

    def key_tables(at):
        labels = labels_ref[group * 8 + at]
        klist_ref[at, 0] = labels.astype(jnp.float32)
        kgain_ref[at] = chosen(sharp, labels, group * 8, 0.0)
        klist_ref[at, 1] = chosen(listed(3 - odd), labels, group * 8, 0.0)
        klist_ref[at, 2] = chosen(listed(2 + odd), labels, group * 8, 0.0)

    lax.fori_loop(0, 8, lambda at, carry: (key_tables(at), carry)[1], 0)
    queries[0] = unit_ref[...]
    keys[dev] = unit_ref[...]
    acc_ref[...] = jnp.zeros_like(acc_ref)
    cols_ref[...] = jnp.zeros_like(cols_ref)

    def first(k):
        side(k).wait_recv()
        relay(k).start()

        @pl.when((z == 1) | (z == 2))
        def _():
            unit = z - 1
            arrived(2 * unit + core, k)
            hop(unit, k, above).start()
            share(unit, k).start()

        @pl.when(z == 2)
        def _():
            arrived(6 + core, k)
            share(3, k).start()

    loop(first)

    def late(k):
        @pl.when(z == 3)
        def _():
            arrived(2 + core, k)
            share(1, k).start()

        relay(k).wait_recv()

    loop(late)

    def stage(k):
        @pl.when(z >= 2)
        def _():
            arrived(core, k)
            share(0, k).start()

        @pl.when(z == 2)
        def _():
            hop(0, k, above).start()

        unit = jnp.where(
            k == 0, z, jnp.where(k == 1, jnp.where(z == 1, 0, 1), jnp.where(k == 2, 3, 0))
        )
        ready = (
            (k == 0)
            | ((k == 1) & (z > 0))
            | ((k == 2) & (z == 2))
            | ((k == PIECES - 1) & (z >= 2))
        )

        @pl.when(ready)
        def _():
            loop(lambda p: arrived(2 * unit + 1 - core, p))
            foreign = jnp.where(k > 0, 1.0, 0.0)

            def one(c, carry):
                at = 2 * unit + c
                products = lax.dot_general(
                    queries[...].reshape(3 * rows, unit_ref.shape[1]),
                    keys[at],
                    (((1,), (1,)), ((), ())),
                    preferred_element_type=jnp.float32,
                )
                down = jnp.zeros((1, rows), jnp.float32)
                kl = klist_ref[at, 0]
                for b in range(3):
                    terms = jnp.exp(
                        0.5 * (gain_ref[b] + kgain_ref[at]) * products[b * rows : (b + 1) * rows]
                    )
                    wanted = lists_ref[b, 1] == kl
                    if b == 0:
                        wanted = wanted | (lists_ref[0, 2] == kl) | (lists_ref[0, 0] == kl)
                        wanted = wanted & jnp.logical_not(same & (at == dev))
                        back = wanted
                    else:
                        back = lists_ref[b, 0] == klist_ref[at, b]
                    acc_ref[b] += jnp.where(wanted, terms, 0.0)
                    down = down + jnp.sum(jnp.where(back, terms, 0.0), axis=0, keepdims=True)
                cols_ref[at] = down * foreign
                return carry

            lax.fori_loop(0, 2, one, 0)

    loop(stage)
    for b in range(3):
        across_lanes = jnp.sum(acc_ref[b], axis=1, keepdims=True)
        rows_ref[b] = jnp.sum(jnp.where(same, across_lanes, 0.0), axis=0, keepdims=True)

    def finish(k):
        own_sends(k, sent)
        sent(relay(k))

        @pl.when((z == 1) | (z == 2))
        def _():
            sent(hop(z - 1, k, above))
            sent(share(z - 1, k))

        @pl.when(z == 2)
        def _():
            sent(share(3, k))
            sent(hop(0, k, above))

        @pl.when(z == 3)
        def _():
            sent(share(1, k))

        @pl.when(z >= 2)
        def _():
            sent(share(0, k))

    loop(finish)


def paired(unit_rows, labels, neighbours, sharpness):
    rows, width = unit_rows.shape
    vmem = pl.BlockSpec(memory_space=pltpu.VMEM)
    smem = pl.BlockSpec(memory_space=pltpu.SMEM)
    return pl.pallas_call(
        pair_kernel,
        out_shape=[
            jax.ShapeDtypeStruct((3, 1, rows), jnp.float32),
            jax.ShapeDtypeStruct((8, 1, rows), jnp.float32),
        ],
        in_specs=[vmem, vmem, smem, smem],
        out_specs=[vmem, vmem],
        scratch_shapes=[
            pltpu.VMEM((3, 3, rows, 1), jnp.float32),
            pltpu.VMEM((3, rows, 1), jnp.float32),
            pltpu.VMEM((8, 3, 1, rows), jnp.float32),
            pltpu.VMEM((8, 1, rows), jnp.float32),
            pltpu.VMEM((3, rows, rows), jnp.float32),
            pltpu.VMEM((3, rows, width), jnp.bfloat16),
            pltpu.VMEM((8, rows, width), jnp.bfloat16),
            pltpu.SemaphoreType.DMA((4, PIECES)),
            pltpu.SemaphoreType.DMA((4, PIECES)),
            pltpu.SemaphoreType.DMA((8, PIECES)),
            pltpu.SemaphoreType.DMA((4, PIECES)),
        ],
        compiler_params=pltpu.CompilerParams(
            collective_id=1, has_side_effects=True, vmem_limit_bytes=56 * 1024 * 1024
        ),
        name="pairs",
    )(unit_rows, labels, neighbours, sharpness)


def lookup(table, index):
    hit = index[:, None] == jnp.arange(table.shape[0], dtype=jnp.int32)[None, :]
    return jnp.sum(jnp.where(hit, table[None, :], jnp.zeros((), table.dtype)), axis=1)


def gathered(documents, cluster_of, neighbours, sharpness):
    groups = lax.axis_size("outer")
    owners = lax.axis_size("dev")
    tokens_here, feature_width = documents.shape
    group_index = lax.axis_index("outer")
    owner_index = lax.axis_index("dev")
    clusters = groups * owners
    cluster_range = jnp.arange(clusters, dtype=jnp.int32)
    sizes = jnp.sum((cluster_of[:, None] == cluster_range[None, :]).astype(jnp.int32), axis=0)

    def labels_at(group_at):
        start = (group_at * owners + owner_index) * tokens_here
        return lax.dynamic_slice_in_dim(cluster_of, start, tokens_here)

    own = labels_at(group_index)
    local = own - group_index * owners
    local_range = jnp.arange(owners, dtype=jnp.int32)
    member = (local_range[:, None] == local[None, :]).astype(jnp.bfloat16)
    sums = summed(jnp.dot(member, documents, preferred_element_type=jnp.float32))
    own_sizes = lax.dynamic_slice_in_dim(sizes, group_index * owners, owners)
    means = sums / own_sizes.astype(jnp.float32)[:, None]
    centre = jnp.dot(
        member.astype(jnp.float32).T,
        means,
        precision=lax.Precision.HIGHEST,
        preferred_element_type=jnp.float32,
    )
    centred = documents.astype(jnp.float32) - centre
    scaling = lax.rsqrt(jnp.mean(centred * centred, axis=1) + 1e-06) / math.sqrt(feature_width)
    unit_rows = (centred * scaling[:, None]).astype(jnp.bfloat16)

    labels = cluster_of.reshape(clusters, 1, tokens_here)
    rows, cols = paired(unit_rows, labels, neighbours, sharpness)
    running = returned(cols, rows)[0]
    counts = sizes - 1
    for position in range(neighbours.shape[1]):
        counts = counts + lookup(sizes, neighbours[:, position])
    return jnp.log(running / lookup(counts, own).astype(jnp.float32))


def solution(mesh):
    small = mesh.shape["dev"] == 8 and mesh.shape["outer"] == 4
    in_specs = (P(("outer", "dev"), None), P(), P(), P())
    out_specs = P(("outer", "dev"))
    body = gathered if small else shards
    return jax.shard_map(body, mesh=mesh, in_specs=in_specs, out_specs=out_specs, check_vma=False)
```

profile of v0, /device:TPU:0, one launch (start us, length us, event | category | flops | bytes accessed | tf_op | source)
XLA Modules:
  0.0 119.5 jit_solution(13956458111869341528)
XLA Ops:
  0.0 0.8 broadcast_subtract_fusion
  0.8 2.4 %fusion.2.part_ref = f32[8,4096]{1,0:T(8,128)} fusion(bf16[192,4096]{1,0:T(8,128)(2,1)} %param.4, s32[192]{0:T(256)S(1)} %get-tuple-element.13), kind=kOutput, calls=%fused_computation.18 | convolution fusion | flops 12584448 | bytes 1704704 | tf_op jit(solution)/shard_map/dot_general | solution.py:538
  3.1 15.6 %mean_sums.1 = f32[8,4096]{1,0:T(8,128)} custom-call(f32[8,4096]{1,0:T(8,128)} %fusion.2.part_ref), custom_call_target="tpu_custom_call" | custom-call | tf_op jit(solution)/shard_map/mean_sums/pallas_call | solution.py:181
  18.7 0.9 convert_reduce_fusion
  19.6 0.1 dynamic-slice_convert_fusion
  19.7 3.3 %multiply_reduce_fusion = (f32[192]{0:T(256)S(1)}, f32[192,4096]{1,0:T(8,128)S(1)}) fusion(f32[8,4096]{1,0:T(8,128)} %mean_sums.1, f32[8]{0:T(128)S(1)} %dynamic-slice_convert_fusion, s32[192]{0:T(256)S(1)} %get-tuple-element.13, bf16[192,4096]{1,0:T(8,128)(2,1)} %param.4), kind=kOutput, calls=%fused_computation.2 | convolution fusion | flops 78677312 | bytes 4851232 | tf_op jit(solution)/shard_map/dot_general | solution.py:541
  23.0 0.0 copy-start
  23.0 0.0 copy-start.1
  23.1 1.5 %multiply_convert_fusion.unit_ref = bf16[192,4096]{1,0:T(8,128)(2,1)} fusion(f32[192,4096]{1,0:T(8,128)S(1)} %get-tuple-element.20, f32[192]{0:T(256)S(1)} %rsqrt_multiply_fusion), kind=kLoop, calls=%fused_computation.1 | loop fusion | flops 1572864 | bytes 4719360 | tf_op jit(solution)/shard_map/convert_element_type | solution.py:549
  24.6 0.0 copy-done
  24.6 0.7 reshape.29.labels_ref
  25.3 0.0 copy-done.1
  25.3 0.7 copy.6.neighbours_ref
  25.9 50.9 %pairs.1 = (f32[3,1,192]{2,1,0:T(1,128)}, f32[8,1,192]{2,1,0:T(1,128)}) custom-call(bf16[192,4096]{1,0:T(8,128)(2,1)} %multiply_convert_fusion.unit_ref, s32[32,1,192]{2,1,0:T(1,128)} %reshape.29.labels_ref, s32[32,4]{1,0:T(8,128)} %copy.6.neighbours_ref, f32[32]{0:T(128)} %sharpness_ref.1), custom_call_target="tpu_custom_call" | custom-call | tf_op jit(solution)/shard_map/pairs/pallas_call | solution.py:487
  76.8 41.1 %return_sums.1 = f32[1,192]{1,0:T(1,128)} custom-call(f32[8,1,192]{2,1,0:T(1,128)} %get-tuple-element.7.cols_ref, f32[3,1,192]{2,1,0:T(1,128)} %get-tuple-element.8.rows_ref), custom_call_target="tpu_custom_call" | custom-call | tf_op jit(solution)/shard_map/return_sums/pallas_call | solution.py:231
  117.9 0.2 select_reduce_fusion.4
  118.2 0.1 select_reduce_fusion
  118.3 1.3 %fusion.5 = f32[192]{0:T(256)} fusion(f32[192]{0:T(256)} %bitcast.10, s32[192]{0:T(256)S(1)} %select_reduce_fusion), kind=kLoop, calls=%fused_computation.23 | loop fusion | flops 384 | bytes 2304 | tf_op jit(solution)/shard_map/log | solution.py:557
  (3 shorter events, 0.0 us)
Async XLA Ops:
  23.0 1.5 %copy-start = (s32[6144]{0:T(1024)S(1)}, s32[6144]{0:T(1024)}, u32[]{:S(2)}) copy-start(s32[6144]{0:T(1024)} %param.5) | copy-start | bytes 73732
  23.0 2.2 %copy-start.1 = (s32[32,4]{0,1:T(4,128)S(1)}, s32[32,4]{0,1:T(4,128)}, u32[]{:S(2)}) copy-start(s32[32,4]{0,1:T(4,128)} %param.6) | copy-start | bytes 1540
where the time goes:
time: 120 us
  Pallas kernels  108 us (90%)
  matrix products  5.66 us (5%)
  other arithmetic  4.84 us (4%)
  local copies, waits for them, and re-layouts  1.39 us (1%)
    pallas_call x1, Pallas kernels, paired(): pl.pallas_call(pair_kernel, out_shape=[jax.ShapeDtypeStruct((3, 1, rows),...  50.9 us
    pallas_call x1, Pallas kernels, returned(): pl.pallas_call(functools.partial(return_kernel, owners), out_shape=jax.Sh...  41.1 us
    pallas_call x1, Pallas kernels, summed(): pl.pallas_call(functools.partial(sum_kernel, owners), out_shape=jax.Shape...  15.6 us
    dot_general x1, matrix products, gathered(): jnp.dot(member.astype(jnp.float32).T, means, precision=lax.Precision.HIGH...  3.3 us

commit v1 on v0

v1 whole, which is shorter than its diff:
```python
import functools
import math

import jax
import jax.numpy as jnp
from jax import lax
from jax.experimental import pallas as pl
from jax.experimental.pallas import tpu as pltpu
from jax.sharding import PartitionSpec as P


def passed_along(block, axis, distance):
    devices = range(lax.axis_size(axis))
    route = [((i - distance) % len(devices), i) for i in devices]
    return lax.ppermute(block, axis, route)


def kernel_block(queries, others, pair_gain):
    products = jnp.einsum("qe,ke->qk", queries, others, preferred_element_type=jnp.float32)
    return jnp.exp(pair_gain * products)


def shards(documents, cluster_of, neighbours, sharpness):
    groups = lax.axis_size("outer")
    owners = lax.axis_size("dev")
    tokens_here = documents.shape[0]
    feature_width = documents.shape[1]
    capacity = max(2, 2 * tokens_here // owners)
    slot_count = owners * capacity
    group_index = lax.axis_index("outer")
    owner_index = lax.axis_index("dev")
    own_cluster = group_index * owners + owner_index
    block_labels = cluster_of.reshape(groups * owners, tokens_here)
    group_of_block = jnp.arange(groups * owners, dtype=jnp.int32) // owners
    local_labels = block_labels - group_of_block[:, None] * owners
    owner_range = jnp.arange(owners, dtype=jnp.int32)
    per_block = jnp.sum(
        (local_labels[:, :, None] == owner_range).astype(jnp.int32), axis=1
    ).reshape(groups, owners, owners)
    cluster_sizes = jnp.sum(per_block, axis=1).reshape(-1)
    own_labels = lax.dynamic_index_in_dim(local_labels, own_cluster, 0, keepdims=False)
    ordinal = jnp.arange(tokens_here, dtype=jnp.int32)
    earlier = ordinal[None, :] < ordinal[:, None]
    repeats = jnp.sum(
        ((own_labels[:, None] == own_labels[None, :]) & earlier).astype(jnp.int32), axis=1
    )
    target = own_labels * capacity + repeats
    placing = (jnp.arange(slot_count, dtype=jnp.int32)[:, None] == target[None, :]).astype(
        jnp.bfloat16
    )
    outgoing = jnp.dot(placing, documents, preferred_element_type=jnp.float32).astype(jnp.bfloat16)
    arrived = lax.all_to_all(
        outgoing.reshape(owners, capacity, feature_width),
        "dev",
        split_axis=0,
        concat_axis=0,
        tiled=True,
    ).reshape(slot_count, feature_width)

    def slot_mask(group_at, owner_at):
        senders = per_block[group_at, :, owner_at]
        return (
            (jnp.arange(capacity, dtype=jnp.int32)[None, :] < senders[:, None])
            .astype(jnp.float32)
            .reshape(-1)
        )

    present = slot_mask(group_index, owner_index)
    centre = jnp.dot(
        present.astype(jnp.bfloat16)[None, :], arrived, preferred_element_type=jnp.float32
    )[0]
    centre = centre / cluster_sizes[own_cluster].astype(jnp.float32)
    centred = arrived.astype(jnp.float32) - centre[None, :]
    scaling = lax.rsqrt(jnp.mean(centred * centred, axis=1) + 1e-06) / math.sqrt(feature_width)
    unit_rows = (centred * (scaling * present)[:, None]).astype(jnp.bfloat16)
    own_gain = sharpness[own_cluster]
    listed = neighbours[own_cluster]
    off_diagonal = 1.0 - jnp.eye(slot_count, dtype=jnp.float32)
    running = jnp.sum(
        kernel_block(unit_rows, unit_rows, own_gain) * (present[None, :] * off_diagonal), axis=1
    )
    beside = [passed_along(unit_rows, "dev", offset) for offset in (1, -1)]
    vertical = []
    for direction, position in ((1, 2), (-1, 3)):
        receiver_group = (group_index + direction) % groups
        wanted = neighbours[receiver_group * owners + owner_index, position]
        delta = (wanted % owners - owner_index + owners) % owners
        picked_rows = jnp.where(
            delta == 1, beside[1], jnp.where(delta == owners - 1, beside[0], unit_rows)
        )
        vertical.append(passed_along(picked_rows, "outer", direction))
    key_sets = [beside[0], beside[1], vertical[0], vertical[1]]
    for position in range(4):
        partner = listed[position]
        partner_group_at = partner // owners
        partner_owner_at = partner % owners
        partner_partner = partner_group_at * owners + partner_owner_at
        pair_gain = 0.5 * (own_gain + sharpness[partner_partner])
        partner = partner_partner
        kernel_terms = kernel_block(unit_rows, key_sets[position], pair_gain)
        key_mask = slot_mask(partner_group_at, partner_owner_at)
        running = running + jnp.sum(kernel_terms * key_mask[None, :], axis=1)
    partner_count = cluster_sizes[own_cluster] - 1 + jnp.sum(cluster_sizes[listed])
    slot_density = jnp.log(running / partner_count.astype(jnp.float32))
    answered = lax.all_to_all(
        slot_density.reshape(owners, capacity), "dev", split_axis=0, concat_axis=0, tiled=True
    ).reshape(-1)
    return answered[target]


MESH = pl.DeviceIdType.MESH


PIECES = 16
GROUPED = 4


def start(copy):
    copy.start()


def sent(copy):
    copy.wait_send()


def landed(copy):
    copy.wait_recv()


def loop(count, body):
    lax.fori_loop(0, count, lambda k, carry: (body(k), carry)[1], 0)


def density_kernel(
    docs_ref, cluster_ref, neighbours_ref, sharpness_ref, out_ref,
    keys, queries, part, pair_half, chip_half, line_in, line_half, middle_in, sums, triple,
    centred, squares, labels_ref, lists_ref, gain_ref, klist_ref, kgain_ref, kscale_ref,
    alpha, products, acc_ref, cols_ref, returned_ref, rows_ref, rows_in,
    load_sems, stage_sems, z_sems, core_sems, key_sems, side_sems, relay_sems, flow_sems,
    scale_sems, return_sems, row_sems,
):
    dev = lax.axis_index("dev")
    group = lax.axis_index("outer")
    z, core = dev // 2, lax.rem(dev, 2)
    odd = lax.rem(group, 2)
    rows, width = docs_ref.shape
    span = width // PIECES
    half = PIECES // 2
    clusters = neighbours_ref.shape[1]
    base = group * 8
    partner_at = 2 * z + 1 - core
    partner = {"dev": partner_at}
    above = {"dev": lax.rem(dev + 2, 8)}
    below = {"dev": lax.rem(dev + 6, 8)}
    beside_group = group + 1 - 2 * odd
    opposite_group = 3 - group
    beside = {"outer": beside_group}
    opposite = {"outer": opposite_group}
    across = {"outer": lax.rem(group + 2, 4)}
    others = [lax.rem(dev + step, 8) for step in range(1, 8)]

    def loading(k):
        return pltpu.make_async_copy(
            docs_ref.at[:, pl.ds(pl.multiple_of(k * span, span), span)],
            keys.at[dev, k],
            load_sems.at[k],
        )

    loop(PIECES, lambda k: loading(k).start())
    barrier = pltpu.get_barrier_semaphore()
    peers = [{"dev": peer} for peer in others] + [beside, opposite, across]
    for peer in peers:
        pl.semaphore_signal(barrier, inc=1, device_id=peer, device_id_type=MESH)

    square = (rows, rows)
    same = lax.broadcasted_iota(jnp.int32, square, 0) == lax.broadcasted_iota(jnp.int32, square, 1)
    lane = lax.broadcasted_iota(jnp.int32, (1, 128), 1)

    def fetch_labels(slot, block):
        top = 3 * (block // 2)
        late = lax.rem(block, 2)
        first = cluster_ref[pl.ds(top, 1), :]
        middle = cluster_ref[pl.ds(top + 1, 1), :]
        last = cluster_ref[pl.ds(top + 2, 1), :]
        turned = jnp.where(lane < 64, pltpu.roll(middle, 64, 1), pltpu.roll(last, 64, 1))
        tail = jnp.where(late == 1, pltpu.roll(last, 64, 1), middle)
        labels_ref[slot, :, 0:128] = jnp.where(late == 1, turned, first)
        labels_ref[slot, :, 128:rows] = tail[:, 0 : rows - 128]

    loop(8, lambda at: fetch_labels(at, base + at))
    fetch_labels(8, beside_group * 8 + dev)
    fetch_labels(9, opposite_group * 8 + dev)
    own_labels = labels_ref[dev]
    member = (
        own_labels == base + lax.broadcasted_iota(jnp.int32, (8, rows), 0)
    ).astype(jnp.bfloat16)

    def partial_sums(k):
        loading(k).wait()
        part[k] = jnp.dot(member, keys[dev, k], preferred_element_type=jnp.float32)

    loop(PIECES, partial_sums)
    pl.semaphore_wait(barrier, len(peers))

    def remote(src, dst, send_sem, recv_sem, device):
        return pltpu.make_async_remote_copy(
            src_ref=src, dst_ref=dst, send_sem=send_sem, recv_sem=recv_sem,
            device_id=device, device_id_type=MESH,
        )

    def hop(unit, k, device):
        at = 2 * unit + core
        return remote(
            keys.at[at, k], keys.at[at, k], z_sems.at[unit], key_sems.at[at, k], device
        )

    def share(unit, k):
        at = 2 * unit + core
        return remote(
            keys.at[at, k], keys.at[at, k], core_sems.at[unit], key_sems.at[at, k], partner
        )

    def whole_sent(unit, sems):
        at = 2 * unit + core
        remote(keys.at[at], keys.at[at], sems.at[unit], key_sems.at[at, 0], partner).wait_send()

    def arrived(at, k):
        remote(
            keys.at[at, k], keys.at[at, k], core_sems.at[0], key_sems.at[at, k], partner
        ).wait_recv()

    def side(k):
        return remote(
            queries.at[k, 0], queries.at[k, 1], flow_sems.at[0], side_sems.at[k], beside
        )

    def relay(k):
        return remote(
            queries.at[k, 1], queries.at[k, 2], flow_sems.at[1], relay_sems.at[k], across
        )

    mine = pl.ds(pl.multiple_of(core * half, half), half)
    theirs = pl.ds(pl.multiple_of((1 - core) * half, half), half)

    def staged(n, src, dst, device):
        return remote(src, dst, stage_sems.at[n, 0], stage_sems.at[n, 1], device)

    pairing = staged(0, part.at[theirs], pair_half, partner)
    lower = staged(1, chip_half, line_in, above)
    upper = staged(1, chip_half, line_in, below)
    rising = staged(2, line_half, middle_in, above)
    sinking = staged(2, line_half, middle_in, below)
    outward_up = staged(3, sums.at[mine], sums.at[mine], above)
    outward_down = staged(3, sums.at[mine], sums.at[mine], below)
    joining = staged(4, sums.at[mine], sums.at[mine], partner)

    def own_hops(first, stop):
        def one(k):
            @pl.when(z < 2)
            def _():
                hop(z, k, above).start()

            @pl.when(z == 3)
            def _():
                hop(z, k, below).start()

        lax.fori_loop(first, stop, lambda k, carry: (one(k), carry)[1], 0)

    pairing.start()
    own_hops(0, 1)

    @pl.when(z == 1)
    def _():
        own_hops(1, 3)

    loop(PIECES, lambda k: share(z, k).start())
    pairing.wait_recv()
    chip_half[...] = part[mine] + pair_half[...]

    @pl.when(z == 0)
    def _():
        lower.start()

    @pl.when(z == 3)
    def _():
        upper.start()

    @pl.when((z == 0) | (z == 3))
    def _():
        own_hops(1, PIECES)

    @pl.when((z == 1) | (z == 2))
    def _():
        lower.wait_recv()
        line_half[...] = chip_half[...] + line_in[...]

        @pl.when(z == 1)
        def _():
            rising.start()
            own_hops(3, PIECES)

        @pl.when(z == 2)
        def _():
            sinking.start()

        rising.wait_recv()
        sums[mine] = line_half[...] + middle_in[...]

        @pl.when(z == 1)
        def _():
            outward_down.start()

        @pl.when(z == 2)
        def _():
            outward_up.start()

    @pl.when((z == 0) | (z == 3))
    def _():
        outward_up.wait_recv()

    joining.start()

    def chosen(read, labels, first, zero):
        found = jnp.full(labels.shape, zero, jnp.float32)
        for h in range(8):
            found = jnp.where(labels == first + h, read(first + h), found)
        return found

    def listed(position):
        return lambda c: neighbours_ref[position, c].astype(jnp.float32)

    def sharp(c):
        return sharpness_ref[c]

    def upright(row):
        return jnp.sum(jnp.where(same, row, 0.0), axis=1, keepdims=True)

    def flat(column):
        return jnp.sum(jnp.where(same, column, 0.0), axis=0, keepdims=True)

    def count_of(c):
        hits = jnp.where(cluster_ref[...] == c, 1.0, 0.0)
        return jnp.sum(jnp.sum(hits, axis=0, keepdims=True), axis=1, keepdims=True)

    own_row = own_labels.astype(jnp.float32)
    own_upright = upright(own_row)
    lists_ref[0, 0] = own_upright
    upright_member = (
        own_upright
        == base.astype(jnp.float32)
        + lax.rem(lax.broadcasted_iota(jnp.int32, (rows, 24), 1), 8).astype(jnp.float32)
    ).astype(jnp.bfloat16)
    local = lax.broadcasted_iota(jnp.int32, (8, 1), 0)
    own_sizes = jnp.zeros((8, 1), jnp.float32)
    for h in range(8):
        own_sizes = jnp.where(local == h, count_of(base + h), own_sizes)

    joining.wait_recv()
    squares[...] = jnp.zeros_like(squares)

    def centre_piece(k):
        means = sums[k] / own_sizes
        high = means.astype(jnp.bfloat16).astype(jnp.float32)
        rest = means - high
        mid = rest.astype(jnp.bfloat16).astype(jnp.float32)
        parts = jnp.concatenate([high, mid, rest - mid], axis=0).astype(jnp.bfloat16)
        triple[k] = parts
        centre = jnp.dot(upright_member, parts, preferred_element_type=jnp.float32)
        moved = keys[dev, k].astype(jnp.float32) - centre
        centred[k] = moved
        squares[...] += moved * moved

    loop(PIECES, centre_piece)
    energy = jnp.sum(squares[...], axis=1, keepdims=True) / width
    scaling = lax.rsqrt(energy + 1e-06) / math.sqrt(width)

    def unit_piece(k):
        queries[k, 0] = (centred[k] * scaling).astype(jnp.bfloat16)

        @pl.when(k > 0)
        def _():
            side(k - 1).start()

    loop(PIECES, unit_piece)
    kscale_ref[dev] = flat(scaling)
    side(PIECES - 1).start()

    def scale_out(n):
        return remote(
            kscale_ref.at[dev], kscale_ref.at[dev],
            scale_sems.at[0, n], scale_sems.at[1, dev], {"dev": others[n]},
        )

    for n in range(7):
        scale_out(n).start()

    def onward(k):
        @pl.when(z == 1)
        def _():
            arrived(core, k)
            hop(0, k, above).start()
            share(0, k).start()

        @pl.when(z == 2)
        def _():
            arrived(6 + core, k)
            hop(3, k, below).start()
            share(3, k).start()
            arrived(2 + core, k)
            share(1, k).start()

    loop(half, onward)

    for b, slot in ((0, dev), (1, 8), (2, 9)):
        first = (base, beside_group * 8, opposite_group * 8)[b]
        labels = labels_ref[slot]
        if b > 0:
            lists_ref[b, 0] = upright(labels.astype(jnp.float32))
        gain_ref[b] = upright(chosen(sharp, labels, first, 0.0))
        positions = ((0, 1), (2 + odd,), (3 - odd,))[b]
        for place, position in enumerate(positions):
            lists_ref[b, 1 + place] = upright(chosen(listed(position), labels, first, 0.0))

    def key_tables(at):
        labels = labels_ref[at]
        klist_ref[at, 0] = labels.astype(jnp.float32)
        kgain_ref[at] = chosen(sharp, labels, base, 0.0)
        klist_ref[at, 1] = chosen(listed(3 - odd), labels, base, 0.0)
        klist_ref[at, 2] = chosen(listed(2 + odd), labels, base, 0.0)

    loop(8, key_tables)
    acc_ref[...] = jnp.zeros_like(acc_ref)
    own_lists = [chosen(listed(position), own_labels, base, 0.0) for position in range(4)]

    def add_count(c, total):
        here = c.astype(jnp.float32)
        found = jnp.where(own_row == here, 1.0, 0.0)
        for row in own_lists:
            found = found + jnp.where(row == here, 1.0, 0.0)
        return total + found * count_of(c)

    partner_count = lax.fori_loop(0, clusters, add_count, jnp.full((1, rows), -1.0, jnp.float32))

    def steps(k):
        side(k).wait_recv()
        relay(k).start()

        @pl.when(k < half)
        def _():
            onward(k + half)

        @pl.when((z == 1) & (k > 1))
        def _():
            arrived(6 + core, k - 2)
            hop(3, k - 2, below).start()
            share(3, k - 2).start()

    loop(PIECES, steps)

    @pl.when(z == 1)
    def _():
        for k in (PIECES - 2, PIECES - 1):
            arrived(6 + core, k)
            hop(3, k, below).start()
            share(3, k).start()

    def late(k):
        relay(k).wait_recv()

        @pl.when(z == 0)
        def _():
            arrived(6 + core, k)
            share(3, k).start()

    loop(PIECES, late)
    contract = (((1,), (1,)), ((), ()))

    def stacked(k):
        return queries[k].reshape(3 * rows, span)

    alpha[...] = jnp.zeros_like(alpha)

    def project(k):
        alpha[...] += lax.dot_general(
            stacked(k), triple[k], contract, preferred_element_type=jnp.float32
        )

    loop(PIECES, project)

    def multiplied(at, k):
        return lax.dot_general(
            stacked(k), keys[at, k], contract, preferred_element_type=jnp.float32
        )

    cluster_24 = base + lax.rem(lax.broadcasted_iota(jnp.int32, (24, rows), 0), 8)

    def finish(at, slot):
        @pl.when(at != dev)
        def _():
            remote(
                kscale_ref.at[at], kscale_ref.at[at],
                scale_sems.at[0, 0], scale_sems.at[1, at], partner,
            ).wait_recv()

        hot = jnp.where(labels_ref[at] == cluster_24, 1.0, 0.0)
        down = jnp.zeros((1, rows), jnp.float32)
        kl = klist_ref[at, 0]
        scale = 0.5 * kscale_ref[at]
        for b in range(3):
            strip = pl.ds(b * rows, rows)
            shift = jnp.dot(
                alpha[strip, :], hot,
                precision=lax.Precision.HIGHEST,
                preferred_element_type=jnp.float32,
            )
            terms = jnp.exp(
                (gain_ref[b] + kgain_ref[at]) * (scale * (products[slot, strip, :] - shift))
            )
            wanted = lists_ref[b, 1] == kl
            if b == 0:
                wanted = wanted | (lists_ref[0, 2] == kl) | (lists_ref[0, 0] == kl)
                wanted = wanted & jnp.logical_not(same & (at == dev))
                back = wanted
            else:
                back = lists_ref[b, 0] == klist_ref[at, b]
            acc_ref[b] += jnp.where(wanted, terms, 0.0)
            down = down + jnp.sum(jnp.where(back, terms, 0.0), axis=0, keepdims=True)
        cols_ref[at] = down

    def give_back(at):
        return remote(
            cols_ref.at[at], returned_ref.at[dev],
            return_sems.at[0, at], return_sems.at[1, dev], {"dev": at},
        )

    def whole_block(at):
        @pl.when(at != dev)
        def _():
            @pl.when(lax.rem(at, 2) != core)
            def _():
                loop(PIECES, lambda k: arrived(at, k))

        def gather(n):
            found = multiplied(at, n * GROUPED)
            for k in range(1, GROUPED):
                found = found + multiplied(at, n * GROUPED + k)
            return found

        products[0] = gather(0)

        def more(n, carry):
            products[0] += gather(n)
            return carry

        lax.fori_loop(1, PIECES // GROUPED, more, 0)
        finish(at, 0)

    def stage(n):
        unit = jnp.where(n == 0, z, jnp.where((n == 1) & (z == 1), 0, jnp.where((n == 1) & (z == 2), 1, 3)))
        ready = (n == 0) | ((n == 1) & (z < 3)) | ((n == 2) & ((z == 1) | (z == 2)))

        @pl.when(ready)
        def _():
            loop(2, lambda c: whole_block(2 * unit + c))

            @pl.when(n > 0)
            def _():
                loop(2, lambda c: give_back(2 * unit + c).start())

    loop(3, stage)

    @pl.when(z == 2)
    def _():
        products[...] = jnp.zeros_like(products)

        def stream(k):
            @pl.when(k < PIECES)
            def _():
                arrived(core, k)
                share(0, k).start()

            @pl.when(k > 0)
            def _():
                products[0] += multiplied(core, k - 1)
                arrived(1 - core, k - 1)
                products[1] += multiplied(1 - core, k - 1)

        loop(PIECES + 1, stream)
        finish(core, 0)
        finish(1 - core, 1)
        loop(2, lambda c: give_back(c).start())

    for b in range(3):
        rows_ref[b] = flat(jnp.sum(acc_ref[b], axis=1, keepdims=True))

    def row_back(b, device):
        return remote(
            rows_ref.at[b], rows_in.at[b - 1], row_sems.at[0, b - 1], row_sems.at[1, b - 1], device
        )

    row_back(1, beside).start()
    row_back(2, opposite).start()

    def came_back(sender):
        remote(
            cols_ref.at[0], returned_ref.at[sender],
            return_sems.at[0, 0], return_sems.at[1, sender], partner,
        ).wait_recv()

    cols_ref[dev] = rows_ref[0]

    def collect(sender):
        unit = sender // 2
        gives = (
            ((z == 0) & ((unit == 1) | (unit == 2)))
            | ((z == 1) & (unit == 2))
            | ((z == 3) & (unit < 3))
        )

        @pl.when(gives)
        def _():
            came_back(sender)
            cols_ref[dev] += returned_ref[sender]

    loop(8, collect)
    row_back(1, beside).wait_recv()
    row_back(2, opposite).wait_recv()
    total = cols_ref[dev] + rows_in[0] + rows_in[1]
    out_ref[...] = jnp.log(total / partner_count)

    pairing.wait_send()
    joining.wait_send()
    whole_sent(z, core_sems)
    remote(queries.at[:, 0], queries.at[:, 1], flow_sems.at[0], side_sems.at[0], beside).wait_send()
    remote(queries.at[:, 1], queries.at[:, 2], flow_sems.at[1], relay_sems.at[0], across).wait_send()
    row_back(1, beside).wait_send()
    row_back(2, opposite).wait_send()
    for n in range(7):
        scale_out(n).wait_send()

    def scale_rest(at):
        unit = at // 2
        used = (
            (unit == z)
            | ((z == 0) & (unit == 3))
            | ((z == 1) & ((unit == 0) | (unit == 3)))
            | ((z == 2) & ((unit == 0) | (unit == 1) | (unit == 3)))
        )

        @pl.when(jnp.logical_not(used))
        def _():
            remote(
                kscale_ref.at[at], kscale_ref.at[at],
                scale_sems.at[0, 0], scale_sems.at[1, at], partner,
            ).wait_recv()

    loop(8, scale_rest)

    def returns_sent(unit):
        loop(2, lambda c: give_back(2 * unit + c).wait_send())

    @pl.when(z != 2)
    def _():
        whole_sent(z, z_sems)

    @pl.when((z == 0) | (z == 3))
    def _():
        lower.wait_send()

    @pl.when((z == 1) | (z == 2))
    def _():
        rising.wait_send()
        outward_up.wait_send()

    @pl.when(z == 0)
    def _():
        whole_sent(3, core_sems)
        returns_sent(3)

    @pl.when(z == 1)
    def _():
        whole_sent(0, z_sems)
        whole_sent(3, z_sems)
        whole_sent(0, core_sems)
        whole_sent(3, core_sems)
        returns_sent(0)
        returns_sent(3)

    @pl.when(z == 2)
    def _():
        whole_sent(3, z_sems)
        for unit in (0, 1, 3):
            whole_sent(unit, core_sems)
            returns_sent(unit)


def gathered(documents, cluster_of, neighbours, sharpness):
    rows, width = documents.shape
    span = width // PIECES
    half = PIECES // 2
    vmem = pl.BlockSpec(memory_space=pltpu.VMEM)
    smem = pl.BlockSpec(memory_space=pltpu.SMEM)
    f32 = functools.partial(pltpu.VMEM, dtype=jnp.float32)
    bf16 = functools.partial(pltpu.VMEM, dtype=jnp.bfloat16)
    sems = pltpu.SemaphoreType.DMA
    density = pl.pallas_call(
        density_kernel,
        out_shape=jax.ShapeDtypeStruct((1, rows), jnp.float32),
        in_specs=[pl.BlockSpec(memory_space=pl.ANY), vmem, smem, smem],
        out_specs=vmem,
        scratch_shapes=[
            bf16((8, PIECES, rows, span)),
            bf16((PIECES, 3, rows, span)),
            f32((PIECES, 8, span)),
            f32((half, 8, span)),
            f32((half, 8, span)),
            f32((half, 8, span)),
            f32((half, 8, span)),
            f32((half, 8, span)),
            f32((PIECES, 8, span)),
            bf16((PIECES, 24, span)),
            f32((PIECES, rows, span)),
            f32((rows, span)),
            pltpu.VMEM((10, 1, rows), jnp.int32),
            f32((3, 3, rows, 1)),
            f32((3, rows, 1)),
            f32((8, 3, 1, rows)),
            f32((8, 1, rows)),
            f32((8, 1, rows)),
            f32((3 * rows, 24)),
            f32((2, 3 * rows, rows)),
            f32((3, rows, rows)),
            f32((8, 1, rows)),
            f32((8, 1, rows)),
            f32((3, 1, rows)),
            f32((2, 1, rows)),
            sems((PIECES,)),
            sems((5, 2)),
            sems((4,)),
            sems((4,)),
            sems((8, PIECES)),
            sems((PIECES,)),
            sems((PIECES,)),
            sems((2,)),
            sems((2, 8)),
            sems((2, 8)),
            sems((2, 2)),
        ],
        compiler_params=pltpu.CompilerParams(
            collective_id=0, has_side_effects=True, vmem_limit_bytes=56 * 1024 * 1024
        ),
        name="density",
    )(documents, cluster_of.reshape(-1, 128), neighbours.T, sharpness)
    return density.reshape(rows)


def solution(mesh):
    small = mesh.shape["dev"] == 8 and mesh.shape["outer"] == 4
    in_specs = (P(("outer", "dev"), None), P(), P(), P())
    out_specs = P(("outer", "dev"))
    body = gathered if small else shards
    return jax.shard_map(body, mesh=mesh, in_specs=in_specs, out_specs=out_specs, check_vma=False)
```

time: 120 us -> 107 us (0.89)
  matrix products: 5.66 us -> 0 us
  other arithmetic: 4.84 us -> 0 us
  Pallas kernels: 108 us -> 106 us
    dot_general x2 -> x0, matrix products: 5.66 us -> none  [the longest x1 3.3 us: gathered(): jnp.dot(member.astype(jnp.float32).T, means, precision=lax.Precision.HIGH...]
    pallas_call x3 -> x1, Pallas kernels: 108 us -> 106 us  [gathered(): pl.pallas_call(density_kernel, out_shape=jax.ShapeDtypeStruct((1, rows),...]
    convert_element_type x2 -> x0, other arithmetic: 1.56 us -> none  [the longest x1 1.49 us: gathered(): unit_rows = (centred * scaling[:, None]).astype(jnp.bfloat16)]
    log x1 -> x0, other arithmetic: 1.26 us -> none  [gathered(): return jnp.log(running / lookup(counts, own).astype(jnp.float32))]
    reduce_sum x3 -> x0, other arithmetic: 1.24 us -> none  [the longest x1 0.92 us: gathered(): jnp.sum((cluster_of[:, None] == cluster_range[None, :]).astype(jnp.int32)...]
where the time goes in v1:
time: 107 us
  Pallas kernels  106 us (99%)
  local copies, waits for them, and re-layouts  1.24 us (1%)
    pallas_call x1, Pallas kernels, gathered(): pl.pallas_call(density_kernel, out_shape=jax.ShapeDtypeStruct((1, rows),...  106 us

profile of v1, /device:TPU:0, one launch (start us, length us, event | category | flops | bytes accessed | tf_op | source)
XLA Modules:
  0.0 107.1 jit_solution(13384031486446317369)
XLA Ops:
  0.0 105.9 %density.1 = f32[1,192]{1,0:T(1,128)} custom-call(bf16[192,4096]{1,0:T(8,128)(2,1)} %docs_ref.1, s32[48,128]{1,0:T(8,128)} %bitcast.3, s32[4,32]{1,0:T(4,128)} %bitcast.5, f32[32]{0:T(128)} %sharpness_ref.1), custom_call_target="tpu_custom_call" | custom-call | tf_op jit(solution)/shard_map/density/pallas_call | solution.py:706
  105.9 1.2 %copy.6 = f32[192]{0:T(256)} copy(f32[192]{0:T(256)} %bitcast.4) | data formatting | bytes 1536

commit v2 on v1

--- a/solution.py
+++ b/solution.py
@@ -135,7 +135,7 @@
     docs_ref, cluster_ref, neighbours_ref, sharpness_ref, out_ref,
     keys, queries, part, pair_half, chip_half, line_in, line_half, middle_in, sums, triple,
     centred, squares, labels_ref, lists_ref, gain_ref, klist_ref, kgain_ref, kscale_ref,
-    alpha, products, acc_ref, cols_ref, returned_ref, rows_ref, rows_in,
+    counts_ref, alpha, alpha_parts, products, acc_ref, cols_ref, returned_ref, rows_ref, rows_in,
     load_sems, stage_sems, z_sems, core_sems, key_sems, side_sems, relay_sems, flow_sems,
     scale_sems, return_sems, row_sems,
 ):
@@ -355,6 +355,10 @@
     for h in range(8):
         own_sizes = jnp.where(local == h, count_of(base + h), own_sizes)
 
+    acc_ref[...] = jnp.zeros_like(acc_ref)
+
+    alpha[...] = jnp.zeros_like(alpha)
+    products[...] = jnp.zeros_like(products)
     joining.wait_recv()
     squares[...] = jnp.zeros_like(squares)
 
@@ -409,92 +413,124 @@
             arrived(2 + core, k)
             share(1, k).start()
 
-    loop(half, onward)
-
-    for b, slot in ((0, dev), (1, 8), (2, 9)):
-        first = (base, beside_group * 8, opposite_group * 8)[b]
-        labels = labels_ref[slot]
-        if b > 0:
-            lists_ref[b, 0] = upright(labels.astype(jnp.float32))
-        gain_ref[b] = upright(chosen(sharp, labels, first, 0.0))
-        positions = ((0, 1), (2 + odd,), (3 - odd,))[b]
-        for place, position in enumerate(positions):
-            lists_ref[b, 1 + place] = upright(chosen(listed(position), labels, first, 0.0))
-
-    def key_tables(at):
-        labels = labels_ref[at]
-        klist_ref[at, 0] = labels.astype(jnp.float32)
-        kgain_ref[at] = chosen(sharp, labels, base, 0.0)
-        klist_ref[at, 1] = chosen(listed(3 - odd), labels, base, 0.0)
-        klist_ref[at, 2] = chosen(listed(2 + odd), labels, base, 0.0)
-
-    loop(8, key_tables)
-    acc_ref[...] = jnp.zeros_like(acc_ref)
-    own_lists = [chosen(listed(position), own_labels, base, 0.0) for position in range(4)]
-
-    def add_count(c, total):
-        here = c.astype(jnp.float32)
-        found = jnp.where(own_row == here, 1.0, 0.0)
-        for row in own_lists:
-            found = found + jnp.where(row == here, 1.0, 0.0)
-        return total + found * count_of(c)
-
-    partner_count = lax.fori_loop(0, clusters, add_count, jnp.full((1, rows), -1.0, jnp.float32))
+    contract = (((1,), (1,)), ((), ()))
+
+    def stacked(k):
+        return queries[k].reshape(3 * rows, span)
+
+    def multiply(at, first, count):
+        found = [
+            lax.dot_general(
+                stacked(first + k), keys[at, first + k], contract,
+                preferred_element_type=jnp.float32,
+            )
+            for k in range(count)
+        ]
+        products[at] += functools.reduce(jnp.add, found)
+
+    early = jnp.where(z == 2, 3, jnp.where(z == 1, 2, 1))
+
+    def early_unit(n):
+        return jnp.where(n == 0, z, jnp.where(n == 2, 3, z - 1))
+
+    def absorb(first):
+        for k in range(GROUPED):
+            relay(first + k).wait_recv()
+        alpha[...] += functools.reduce(
+            jnp.add,
+            [
+                lax.dot_general(
+                    stacked(first + k), triple[first + k], contract,
+                    preferred_element_type=jnp.float32,
+                )
+                for k in range(GROUPED)
+            ],
+        )
+
+    def consume(n, first):
+        unit = early_unit(n)
+        multiply(2 * unit + core, first, GROUPED)
+        for k in range(GROUPED):
+            arrived(2 * unit + 1 - core, first + k)
+        multiply(2 * unit + 1 - core, first, GROUPED)
+
+    def query_tables():
+        for b, slot in ((0, dev), (1, 8), (2, 9)):
+            first = (base, beside_group * 8, opposite_group * 8)[b]
+            labels = labels_ref[slot]
+            if b > 0:
+                lists_ref[b, 0] = upright(labels.astype(jnp.float32))
+            gain_ref[b] = upright(chosen(sharp, labels, first, 0.0))
+            positions = ((0, 1), (2 + odd,), (3 - odd,))[b]
+            for place, position in enumerate(positions):
+                lists_ref[b, 1 + place] = upright(chosen(listed(position), labels, first, 0.0))
+
+    def all_key_tables():
+        def key_tables(at):
+            labels = labels_ref[at]
+            klist_ref[at, 0] = labels.astype(jnp.float32)
+            kgain_ref[at] = chosen(sharp, labels, base, 0.0)
+            klist_ref[at, 1] = chosen(listed(3 - odd), labels, base, 0.0)
+            klist_ref[at, 2] = chosen(listed(2 + odd), labels, base, 0.0)
+
+        loop(8, key_tables)
+    def count_table():
+        own_lists = [chosen(listed(position), own_labels, base, 0.0) for position in range(4)]
+
+        def add_count(c, total):
+            here = c.astype(jnp.float32)
+            found = jnp.where(own_row == here, 1.0, 0.0)
+            for row in own_lists:
+                found = found + jnp.where(row == here, 1.0, 0.0)
+            return total + found * count_of(c)
+
+        counts_ref[...] = lax.fori_loop(0, clusters, add_count, jnp.full((1, rows), -1.0, jnp.float32))
 
     def steps(k):
-        side(k).wait_recv()
-        relay(k).start()
+        @pl.when(k < PIECES)
+        def _():
+            side(k).wait_recv()
+            relay(k).start()
 
         @pl.when(k < half)
         def _():
-            onward(k + half)
-
-        @pl.when((z == 1) & (k > 1))
+            onward(2 * k)
+            onward(2 * k + 1)
+
+        @pl.when((z == 1) & (k > 1) & (k < PIECES + 2))
         def _():
             arrived(6 + core, k - 2)
             hop(3, k - 2, below).start()
             share(3, k - 2).start()
 
-    loop(PIECES, steps)
-
-    @pl.when(z == 1)
-    def _():
-        for k in (PIECES - 2, PIECES - 1):
-            arrived(6 + core, k)
-            hop(3, k, below).start()
-            share(3, k).start()
-
-    def late(k):
-        relay(k).wait_recv()
-
-        @pl.when(z == 0)
-        def _():
-            arrived(6 + core, k)
-            share(3, k).start()
-
-    loop(PIECES, late)
-    contract = (((1,), (1,)), ((), ()))
-
-    def stacked(k):
-        return queries[k].reshape(3 * rows, span)
-
-    alpha[...] = jnp.zeros_like(alpha)
-
-    def project(k):
-        alpha[...] += lax.dot_general(
-            stacked(k), triple[k], contract, preferred_element_type=jnp.float32
-        )
-
-    loop(PIECES, project)
-
-    def multiplied(at, k):
-        return lax.dot_general(
-            stacked(k), keys[at, k], contract, preferred_element_type=jnp.float32
-        )
-
-    cluster_24 = base + lax.rem(lax.broadcasted_iota(jnp.int32, (24, rows), 0), 8)
-
-    def finish(at, slot):
+        for when, table in ((1, query_tables), (2, all_key_tables), (3, count_table)):
+            pl.when(k == when)(table)
+
+        turn = lax.rem(k - 1, GROUPED)
+        first = k - 1 - turn - GROUPED
+
+        @pl.when((first >= 0) & (turn == 0))
+        def _():
+            absorb(first)
+
+        @pl.when((first >= 0) & (turn < early))
+        def _():
+            consume(turn, first)
+
+    loop(PIECES + GROUPED, steps)
+    high = alpha[...].astype(jnp.bfloat16)
+    rest = alpha[...] - high.astype(jnp.float32)
+    mid = rest.astype(jnp.bfloat16)
+    alpha_parts[:, 0:24] = high
+    alpha_parts[:, 24:48] = mid
+    alpha_parts[:, 48:72] = (rest - mid.astype(jnp.float32)).astype(jnp.bfloat16)
+    cluster_of_part = base + lax.rem(lax.broadcasted_iota(jnp.int32, (72, rows), 0), 8)
+
+    def settle(at):
+        hot = (labels_ref[at] == cluster_of_part).astype(jnp.bfloat16)
+        products[at] -= jnp.dot(alpha_parts[...], hot, preferred_element_type=jnp.float32)
+
+    def finish(at):
         @pl.when(at != dev)
         def _():
             remote(
@@ -502,19 +538,12 @@
                 scale_sems.at[0, 0], scale_sems.at[1, at], partner,
             ).wait_recv()
 
-        hot = jnp.where(labels_ref[at] == cluster_24, 1.0, 0.0)
         down = jnp.zeros((1, rows), jnp.float32)
         kl = klist_ref[at, 0]
         scale = 0.5 * kscale_ref[at]
         for b in range(3):
-            strip = pl.ds(b * rows, rows)
-            shift = jnp.dot(
-                alpha[strip, :], hot,
-                precision=lax.Precision.HIGHEST,
-                preferred_element_type=jnp.float32,
-            )
             terms = jnp.exp(
-                (gain_ref[b] + kgain_ref[at]) * (scale * (products[slot, strip, :] - shift))
+                (gain_ref[b] + kgain_ref[at]) * (scale * products[at, pl.ds(b * rows, rows), :])
             )
             wanted = lists_ref[b, 1] == kl
             if b == 0:
@@ -533,73 +562,57 @@
             return_sems.at[0, at], return_sems.at[1, dev], {"dev": at},
         )
 
-    def whole_block(at):
-        @pl.when(at != dev)
-        def _():
-            @pl.when(lax.rem(at, 2) != core)
+    def finish_early(n):
+        unit = early_unit(n)
+
+        def one(c):
+            settle(2 * unit + c)
+            finish(2 * unit + c)
+
+        loop(2, one)
+
+        @pl.when(n > 0)
+        def _():
+            loop(2, lambda c: give_back(2 * unit + c).start())
+
+    loop(early, finish_early)
+
+    @pl.when(z < 3)
+    def _():
+        unit = jnp.where(z == 2, 0, 3)
+        ours, other = 2 * unit + core, 2 * unit + 1 - core
+        settle(ours)
+        settle(other)
+
+        def stream(first, count):
+            @pl.when(z != 1)
             def _():
-                loop(PIECES, lambda k: arrived(at, k))
-
-        def gather(n):
-            found = multiplied(at, n * GROUPED)
-            for k in range(1, GROUPED):
-                found = found + multiplied(at, n * GROUPED + k)
-            return found
-
-        products[0] = gather(0)
-
-        def more(n, carry):
-            products[0] += gather(n)
-            return carry
-
-        lax.fori_loop(1, PIECES // GROUPED, more, 0)
-        finish(at, 0)
-
-    def stage(n):
-        unit = jnp.where(n == 0, z, jnp.where((n == 1) & (z == 1), 0, jnp.where((n == 1) & (z == 2), 1, 3)))
-        ready = (n == 0) | ((n == 1) & (z < 3)) | ((n == 2) & ((z == 1) | (z == 2)))
-
-        @pl.when(ready)
-        def _():
-            loop(2, lambda c: whole_block(2 * unit + c))
-
-            @pl.when(n > 0)
-            def _():
-                loop(2, lambda c: give_back(2 * unit + c).start())
-
-    loop(3, stage)
-
-    @pl.when(z == 2)
-    def _():
-        products[...] = jnp.zeros_like(products)
-
-        def stream(k):
-            @pl.when(k < PIECES)
-            def _():
-                arrived(core, k)
-                share(0, k).start()
-
-            @pl.when(k > 0)
-            def _():
-                products[0] += multiplied(core, k - 1)
-                arrived(1 - core, k - 1)
-                products[1] += multiplied(1 - core, k - 1)
-
-        loop(PIECES + 1, stream)
-        finish(core, 0)
-        finish(1 - core, 1)
-        loop(2, lambda c: give_back(c).start())
-
-    for b in range(3):
-        rows_ref[b] = flat(jnp.sum(acc_ref[b], axis=1, keepdims=True))
+                for k in range(count):
+                    arrived(ours, first + k)
+                    share(unit, first + k).start()
+
+            multiply(ours, first, count)
+            for k in range(count):
+                arrived(other, first + k)
+            multiply(other, first, count)
+
+        loop(PIECES // GROUPED - 1, lambda g: stream(g * GROUPED, GROUPED))
+        stream(PIECES - GROUPED, GROUPED - 1)
+        stream(PIECES - 1, 1)
+        finish(ours)
+        give_back(ours).start()
+        finish(other)
+        give_back(other).start()
 
     def row_back(b, device):
         return remote(
             rows_ref.at[b], rows_in.at[b - 1], row_sems.at[0, b - 1], row_sems.at[1, b - 1], device
         )
 
-    row_back(1, beside).start()
-    row_back(2, opposite).start()
+    for b in (2, 1, 0):
+        rows_ref[b] = flat(jnp.sum(acc_ref[b], axis=1, keepdims=True))
+        if b > 0:
+            row_back(b, {1: beside, 2: opposite}[b]).start()
 
     def came_back(sender):
         remote(
@@ -626,7 +639,7 @@
     row_back(1, beside).wait_recv()
     row_back(2, opposite).wait_recv()
     total = cols_ref[dev] + rows_in[0] + rows_in[1]
-    out_ref[...] = jnp.log(total / partner_count)
+    out_ref[...] = jnp.log(total / counts_ref[...])
 
     pairing.wait_send()
     joining.wait_send()
@@ -727,8 +740,10 @@
             f32((8, 3, 1, rows)),
             f32((8, 1, rows)),
             f32((8, 1, rows)),
+            f32((1, rows)),
             f32((3 * rows, 24)),
-            f32((2, 3 * rows, rows)),
+            bf16((3 * rows, 72)),
+            f32((8, 3 * rows, rows)),
             f32((3, rows, rows)),
             f32((8, 1, rows)),
             f32((8, 1, rows)),

time: 107 us -> 91.6 us (0.86)
  Pallas kernels: 106 us -> 90.2 us
    pallas_call x1, Pallas kernels: 106 us -> 90.2 us  [gathered(): pl.pallas_call(density_kernel, out_shape=jax.ShapeDtypeStruct((1, rows),...]
where the time goes in v2:
time: 91.6 us; the launch traced here: 91.4 us
  Pallas kernels  90.2 us (98%)
  local copies, waits for them, and re-layouts  1.24 us (1%)
    pallas_call x1, Pallas kernels, gathered(): pl.pallas_call(density_kernel, out_shape=jax.ShapeDtypeStruct((1, rows),...  90.2 us

profile of v2, /device:TPU:0, one launch (start us, length us, event | category | flops | bytes accessed | tf_op | source)
XLA Modules:
  0.0 91.4 jit_solution(4078327209792110849)
XLA Ops:
  0.0 90.2 %density.1 = f32[1,192]{1,0:T(1,128)} custom-call(bf16[192,4096]{1,0:T(8,128)(2,1)} %docs_ref.1, s32[48,128]{1,0:T(8,128)} %bitcast.3, s32[4,32]{1,0:T(4,128)} %bitcast.5, f32[32]{0:T(128)} %sharpness_ref.1), custom_call_target="tpu_custom_call" | custom-call | tf_op jit(solution)/shard_map/density/pallas_call | solution.py:719
  90.2 1.2 %copy.6 = f32[192]{0:T(256)} copy(f32[192]{0:T(256)} %bitcast.4) | data formatting | bytes 1536

commit v3 on v2

--- a/solution.py
+++ b/solution.py
@@ -256,7 +256,7 @@
 
     def own_hops(first, stop):
         def one(k):
-            @pl.when(z < 2)
+            @pl.when(z < 3)
             def _():
                 hop(z, k, above).start()
 
@@ -267,7 +267,10 @@
         lax.fori_loop(first, stop, lambda k, carry: (one(k), carry)[1], 0)
 
     pairing.start()
-    own_hops(0, 1)
+
+    @pl.when(z != 2)
+    def _():
+        own_hops(0, 1)
 
     @pl.when(z == 1)
     def _():
@@ -313,6 +316,7 @@
         @pl.when(z == 2)
         def _():
             outward_up.start()
+            own_hops(0, PIECES)
 
     @pl.when((z == 0) | (z == 3))
     def _():
@@ -409,7 +413,6 @@
         def _():
             arrived(6 + core, k)
             hop(3, k, below).start()
-            share(3, k).start()
             arrived(2 + core, k)
             share(1, k).start()
 
@@ -428,10 +431,10 @@
         ]
         products[at] += functools.reduce(jnp.add, found)
 
-    early = jnp.where(z == 2, 3, jnp.where(z == 1, 2, 1))
+    early = jnp.where(z > 0, 2, 1)
 
     def early_unit(n):
-        return jnp.where(n == 0, z, jnp.where(n == 2, 3, z - 1))
+        return z - n
 
     def absorb(first):
         for k in range(GROUPED):
@@ -454,6 +457,21 @@
             arrived(2 * unit + 1 - core, first + k)
         multiply(2 * unit + 1 - core, first, GROUPED)
 
+    last = jnp.where(z == 2, 0, 3)
+    ours, other = 2 * last + core, 2 * last + 1 - core
+
+    def stream(first, count):
+        @pl.when(z != 1)
+        def _():
+            for k in range(count):
+                arrived(ours, first + k)
+                share(last, first + k).start()
+
+        multiply(ours, first, count)
+        for k in range(count):
+            arrived(other, first + k)
+        multiply(other, first, count)
+
     def query_tables():
         for b, slot in ((0, dev), (1, 8), (2, 9)):
             first = (base, beside_group * 8, opposite_group * 8)[b]
@@ -497,6 +515,11 @@
             onward(2 * k)
             onward(2 * k + 1)
 
+        @pl.when((z == 3) & (k < PIECES))
+        def _():
+            arrived(4 + core, k)
+            share(2, k).start()
+
         @pl.when((z == 1) & (k > 1) & (k < PIECES + 2))
         def _():
             arrived(6 + core, k - 2)
@@ -516,6 +539,10 @@
         @pl.when((first >= 0) & (turn < early))
         def _():
             consume(turn, first)
+
+        @pl.when((z == 2) & (k == PIECES - 1))
+        def _():
+            stream(0, GROUPED)
 
     loop(PIECES + GROUPED, steps)
     high = alpha[...].astype(jnp.bfloat16)
@@ -579,24 +606,13 @@
 
     @pl.when(z < 3)
     def _():
-        unit = jnp.where(z == 2, 0, 3)
-        ours, other = 2 * unit + core, 2 * unit + 1 - core
         settle(ours)
         settle(other)
 
-        def stream(first, count):
-            @pl.when(z != 1)
-            def _():
-                for k in range(count):
-                    arrived(ours, first + k)
-                    share(unit, first + k).start()
-
-            multiply(ours, first, count)
-            for k in range(count):
-                arrived(other, first + k)
-            multiply(other, first, count)
-
-        loop(PIECES // GROUPED - 1, lambda g: stream(g * GROUPED, GROUPED))
+        lax.fori_loop(
+            jnp.where(z == 2, 1, 0), PIECES // GROUPED - 1,
+            lambda g, carry: (stream(g * GROUPED, GROUPED), carry)[1], 0,
+        )
         stream(PIECES - GROUPED, GROUPED - 1)
         stream(PIECES - 1, 1)
         finish(ours)
@@ -627,7 +643,8 @@
         gives = (
             ((z == 0) & ((unit == 1) | (unit == 2)))
             | ((z == 1) & (unit == 2))
-            | ((z == 3) & (unit < 3))
+            | ((z == 2) & (unit == 3))
+            | ((z == 3) & (unit < 2))
         )
 
         @pl.when(gives)
@@ -657,7 +674,8 @@
             (unit == z)
             | ((z == 0) & (unit == 3))
             | ((z == 1) & ((unit == 0) | (unit == 3)))
-            | ((z == 2) & ((unit == 0) | (unit == 1) | (unit == 3)))
+            | ((z == 2) & (unit < 2))
+            | ((z == 3) & (unit == 2))
         )
 
         @pl.when(jnp.logical_not(used))
@@ -672,9 +690,7 @@
     def returns_sent(unit):
         loop(2, lambda c: give_back(2 * unit + c).wait_send())
 
-    @pl.when(z != 2)
-    def _():
-        whole_sent(z, z_sems)
+    whole_sent(z, z_sems)
 
     @pl.when((z == 0) | (z == 3))
     def _():
@@ -702,9 +718,14 @@
     @pl.when(z == 2)
     def _():
         whole_sent(3, z_sems)
-        for unit in (0, 1, 3):
+        for unit in (0, 1):
             whole_sent(unit, core_sems)
             returns_sent(unit)
+
+    @pl.when(z == 3)
+    def _():
+        whole_sent(2, core_sems)
+        returns_sent(2)
 
 
 def gathered(documents, cluster_of, neighbours, sharpness):

time: 91.6 us -> 86.3 us (0.942)
  Pallas kernels: 90.2 us -> 84.9 us
    pallas_call x1, Pallas kernels: 90.2 us -> 84.9 us  [gathered(): pl.pallas_call(density_kernel, out_shape=jax.ShapeDtypeStruct((1, rows),...]
where the time goes in v3:
time: 86.3 us; the launch traced here: 86.1 us
  Pallas kernels  84.9 us (98%)
  local copies, waits for them, and re-layouts  1.24 us (1%)
    pallas_call x1, Pallas kernels, gathered(): pl.pallas_call(density_kernel, out_shape=jax.ShapeDtypeStruct((1, rows),...  84.9 us

profile of v3, /device:TPU:0, one launch (start us, length us, event | category | flops | bytes accessed | tf_op | source)
XLA Modules:
  0.0 86.1 jit_solution(16446168496725896462)
XLA Ops:
  0.0 84.9 %density.1 = f32[1,192]{1,0:T(1,128)} custom-call(bf16[192,4096]{1,0:T(8,128)(2,1)} %docs_ref.1, s32[48,128]{1,0:T(8,128)} %bitcast.3, s32[4,32]{1,0:T(4,128)} %bitcast.5, f32[32]{0:T(128)} %sharpness_ref.1), custom_call_target="tpu_custom_call" | custom-call | tf_op jit(solution)/shard_map/density/pallas_call | solution.py:740
  84.9 1.2 %copy.6 = f32[192]{0:T(256)} copy(f32[192]{0:T(256)} %bitcast.4) | data formatting | bytes 1536
